TPU v7x, 128 devices: a whole 4x4x4 slice. The times are simulated.
128 devices in a mesh: node: 8 (over x, core), local: 16 (over y, z).
Axes of the slice: x: 4, y: 4, z: 4, core: 2. Of those that a mesh axis runs over, the one named last changes fastest.
Arguments:
- tokens: bfloat16 [2048, 7168], P('node', 'local'), may hold values from -6 to 6
- grad_out: bfloat16 [2048, 7168], P('node', 'local'), may hold values from -0.59765625 to 0.59765625
- gates: bfloat16 [2048, 8], P('node'), may hold values from 0.05 to 10
- routes: int32 [2048, 8], P('node'), may hold values from 0 to 31, all different within a row; in each aligned block of 256 rows (0 to 255, 256 to 511, ...) at most 80 rows name the same one
- w_gate: bfloat16 [32, 7168, 1024], P('node', 'local'), may hold values from -0.09375 to 0.09375
- w_up: bfloat16 [32, 7168, 1024], P('node', 'local'), may hold values from -0.09375 to 0.09375
- w_down: bfloat16 [32, 1024, 7168], P('node', None, 'local'), may hold values from -0.25 to 0.25
Outputs:
- grad_tokens: bfloat16 [2048, 7168], P('node', 'local')
- grad_gates: bfloat16 [2048, 8], P('node')
- grad_w_gate: bfloat16 [32, 7168, 1024], P('node', 'local')
- grad_w_up: bfloat16 [32, 7168, 1024], P('node', 'local')
- grad_w_down: bfloat16 [32, 1024, 7168], P('node', None, 'local')
- loads: float32 [32], replicated
Inputs may be any that keep to these rules, and one draw needn't show every extreme that they name: `routes`: each row names 8 different experts. Within each aligned block of 256 rows (the rows of one index of node) no expert is named by more than 80 rows, and in some blocks one expert is named by exactly 80 rows.
All inputs are finite; a program needn't handle non-finite values.
Results may differ from a plain program's by a relative error of at most 0.033.
Values may be sent and summed in bfloat16 or wider, within the bound.
No kernel may reach another device: no remote copies, remote signals or barrier semaphores. Data moves between devices by JAX's collectives and lax.ppermute only.
A program may use at most 128 MiB of HBM per device.

v0:
```python
import jax
import jax.numpy as jnp
from jax import lax
from jax.sharding import PartitionSpec as P


def copy_for_each(array, axis):
    devices = lax.axis_size(axis)
    return lax.all_to_all(
        jnp.broadcast_to(array[None], (devices, *array.shape)), axis, 0, 0, tiled=True
    )


def over_copies(array, axis):
    return copy_for_each(array, axis).sum(axis=0)


def activation_grads(gate_pre, up_pre, back_hidden, gate_col):
    logistic = jax.nn.sigmoid(gate_pre)
    swished = gate_pre * logistic
    hidden = swished * up_pre
    products = jnp.sum(hidden * back_hidden, axis=-1)
    weight_col = gate_col.astype(jnp.float32)
    scaled = weight_col * back_hidden
    grad_up = (scaled * swished).astype(jnp.bfloat16)
    grad_gate = (scaled * up_pre * logistic * (1.0 + gate_pre * (1.0 - logistic))).astype(
        jnp.bfloat16
    )
    weighted = (weight_col * hidden).astype(jnp.bfloat16)
    return (weighted, grad_gate, grad_up, products)


def slot_tables(flat_routes, flat_gates, expert_count, capacity):
    experts_row = jnp.arange(expert_count, dtype=jnp.int32)
    onehot = (flat_routes[..., None] == experts_row).astype(jnp.int32)
    before = jnp.cumsum(onehot, axis=-2) - onehot
    slot_index = jnp.sum(before * onehot, axis=-1)
    target = flat_routes * capacity + slot_index
    weight_sum = jnp.sum(
        onehot.astype(jnp.float32) * flat_gates.astype(jnp.float32)[:, None], axis=0
    )
    return (target, weight_sum)


def on_device(tokens, grad_out, gates, routes, w_gate, w_up, w_down):
    node_count = lax.axis_size("node")
    tok_node, width_local = tokens.shape
    top_k = routes.shape[1]
    exp_node = w_gate.shape[0]
    experts = exp_node * node_count
    capacity = 5 * tok_node * top_k // (4 * experts)
    flat_routes = routes.reshape(tok_node * top_k)
    flat_gates = gates.reshape(tok_node * top_k)
    target, weight_sum = slot_tables(flat_routes, flat_gates, experts, capacity)
    summed = over_copies(weight_sum, "node")
    loads = summed * (experts / (tok_node * top_k))
    owners = jnp.arange(tok_node * top_k, dtype=jnp.int32) // top_k
    token_of = jnp.full((experts * capacity,), tok_node, jnp.int32).at[target].set(owners)
    gate_of = jnp.zeros((experts * capacity,), jnp.bfloat16).at[target].set(flat_gates)
    zero_row = jnp.zeros((1, width_local), jnp.bfloat16)
    send_tokens = jnp.concatenate([tokens, zero_row], 0)[token_of].reshape(
        node_count, exp_node, capacity, width_local
    )
    send_grads = jnp.concatenate([grad_out, zero_row], 0)[token_of].reshape(
        node_count, exp_node, capacity, width_local
    )
    send_gates = gate_of.reshape(node_count, exp_node, capacity)
    token_rows, grad_rows, gate_rows = (
        lax.all_to_all(send_tokens, "node", split_axis=0, concat_axis=0, tiled=True),
        lax.all_to_all(send_grads, "node", split_axis=0, concat_axis=0, tiled=True),
        lax.all_to_all(send_gates, "node", split_axis=0, concat_axis=0, tiled=True),
    )
    gate_pre = jnp.einsum("sjcd,jdh->sjch", token_rows, w_gate, preferred_element_type=jnp.float32)
    up_pre = jnp.einsum("sjcd,jdh->sjch", token_rows, w_up, preferred_element_type=jnp.float32)
    back_hidden = jnp.einsum(
        "sjcd,jhd->sjch", grad_rows, w_down, preferred_element_type=jnp.float32
    )
    gate_col = gate_rows[..., None]
    gate_full, up_full, back_full = (
        lax.psum(gate_pre.astype(jnp.bfloat16), "local").astype(jnp.float32),
        lax.psum(up_pre.astype(jnp.bfloat16), "local").astype(jnp.float32),
        lax.psum(back_hidden.astype(jnp.bfloat16), "local").astype(jnp.float32),
    )
    weighted, grad_gate, grad_up, products = activation_grads(
        gate_full, up_full, back_full, gate_col
    )
    grad_wg = jnp.einsum(
        "sjcd,sjch->jdh", token_rows, grad_gate, preferred_element_type=jnp.float32
    ).astype(jnp.bfloat16)
    grad_wu = jnp.einsum(
        "sjcd,sjch->jdh", token_rows, grad_up, preferred_element_type=jnp.float32
    ).astype(jnp.bfloat16)
    grad_wd = jnp.einsum(
        "sjch,sjcd->jhd", weighted, grad_rows, preferred_element_type=jnp.float32
    ).astype(jnp.bfloat16)
    input_rows = (
        jnp.einsum("sjch,jdh->sjcd", grad_gate, w_gate, preferred_element_type=jnp.float32)
        + jnp.einsum("sjch,jdh->sjcd", grad_up, w_up, preferred_element_type=jnp.float32)
    ).astype(jnp.bfloat16)
    returned_rows = lax.all_to_all(input_rows, "node", split_axis=0, concat_axis=0, tiled=True)
    returned_products = lax.all_to_all(
        products.astype(jnp.bfloat16), "node", split_axis=0, concat_axis=0, tiled=True
    )
    picked = returned_rows.reshape(experts * capacity, width_local)[target].reshape(
        tok_node, top_k, width_local
    )
    grad_tokens = jnp.sum(picked.astype(jnp.float32), axis=1).astype(jnp.bfloat16)
    grad_gates = returned_products.reshape(experts * capacity)[target].reshape(tok_node, top_k)
    return (grad_tokens, grad_gates, grad_wg, grad_wu, grad_wd, loads)


def solution(mesh):
    in_specs = (
        P("node", "local"),
        P("node", "local"),
        P("node", None),
        P("node", None),
        P("node", "local", None),
        P("node", "local", None),
        P("node", None, "local"),
    )
    out_specs = (
        P("node", "local"),
        P("node", None),
        P("node", "local", None),
        P("node", "local", None),
        P("node", None, "local"),
        P(),
    )
    return jax.shard_map(
        on_device, mesh=mesh, in_specs=in_specs, out_specs=out_specs, check_vma=False
    )
```

profile of v0, /device:TPU:1, one launch (start us, length us, event | category | flops | bytes accessed | tf_op | source)
XLA Modules:
  0.0 423.8 jit_solution(13663327641786896091)
XLA Ops:
  8.9 9.1 %reduce-window.6 = s32[32,16,128]{2,1,0:T(8,128)S(1)} reduce-window(s32[32,16,128]{2,1,0:T(8,128)S(1)} %fusion.47, s32[]{:T(128)} %constant.32.clone.1), window={size=1x1x128 pad=0_0x0_0x127_0}, to_apply=%region_0.0 | reduce-window | flops 8323072 | bytes 524292 | tf_op jit(solution)/shard_map/reduce-window
  19.1 8.1 %scatter_custom_fusion.1 = s32[2560]{0:T(1024)S(1)} fusion(s32[2048]{0:T(1024)S(1)} %bitcast.73, s32[2048]{0:T(1024)S(1)} %add_select_fusion, s32[]{:T(128)} %constant.34.clone.1), kind=kCustom, calls=%fused_computation.75 | custom fusion | bytes 10244 | tf_op jit(solution)/shard_map/scatter | solution.py:58
  28.3 8.2 %gather_fusion.1 = bf16[2560,448]{1,0:T(8,128)(2,1)} fusion(bf16[257,448]{1,0:T(8,128)(2,1)S(1)} %concatenate.7, s32[3072]{0:T(1024)S(1)} %pad_clamp_fusion), kind=kCustom, calls=%fused_computation.1 | custom fusion | bytes 4597760 | tf_op jit(solution)/shard_map/gather | solution.py:61
  36.5 5.9 %all-to-all-start.2 = ((bf16[8,4,80,448]{3,2,1,0:T(8,128)(2,1)}), bf16[8,4,80,448]{3,2,1,0:T(8,128)(2,1)S(1)}, u32[]{:S(2)}, u32[]{:S(2)}) async-start(bf16[8,4,80,448]{3,2,1,0:T(8,128)(2,1)} %bitcast.9), calls=%async_computation.2 | async-start | bytes 5242880 | tf_op jit(solution)/shard_map/all_to_all | solution.py:69
  42.6 8.2 %gather_fusion = bf16[2560,448]{1,0:T(8,128)(2,1)} fusion(bf16[257,448]{1,0:T(8,128)(2,1)S(1)} %concatenate.6, s32[3072]{0:T(1024)S(1)} %pad_clamp_fusion), kind=kCustom, calls=%fused_computation | custom fusion | bytes 4597760 | tf_op jit(solution)/shard_map/gather | solution.py:64
  50.8 23.4 %all-to-all-done.2 = bf16[8,4,80,448]{3,2,1,0:T(8,128)(2,1)S(1)} async-done(((bf16[8,4,80,448]{3,2,1,0:T(8,128)(2,1)}), bf16[8,4,80,448]{3,2,1,0:T(8,128)(2,1)S(1)}, u32[]{:S(2)}, u32[]{:S(2)}) %all-to-all-start.2) | async-done | bytes 2293792 | tf_op jit(solution)/shard_map/all_to_all | solution.py:69
  74.3 5.3 %all-to-all-start.1 = ((bf16[8,4,80,448]{3,2,1,0:T(8,128)(2,1)}), bf16[8,4,80,448]{3,2,1,0:T(8,128)(2,1)}, u32[]{:S(2)}, u32[]{:S(2)}) async-start(bf16[8,4,80,448]{3,2,1,0:T(8,128)(2,1)} %bitcast.5), calls=%async_computation.1 | async-start | bytes 5242880 | tf_op jit(solution)/shard_map/all_to_all | solution.py:70
  79.6 6.8 %convert_bitcast_fusion = bf16[8,4,80,1024]{3,2,0,1:T(8,128)(2,1)} fusion(bf16[4,448,1024]{2,1,0:T(8,128)(2,1)} %param.11, bf16[8,4,80,448]{3,2,1,0:T(8,128)(2,1)S(1)} %all-to-all-done.2), kind=kOutput, calls=%fused_computation.33 | convolution fusion | flops 2351431680 | bytes 11206656 | tf_op jit(solution)/shard_map/sjcd,jdh->sjch/dot_general | solution.py:73
  86.4 4.6 %convert_bitcast_fusion.1 = bf16[8,4,80,1024]{3,2,0,1:T(8,128)(2,1)} fusion(bf16[4,448,1024]{2,1,0:T(8,128)(2,1)S(1)} %copy-done.6, bf16[8,4,80,448]{3,2,1,0:T(8,128)(2,1)S(1)} %all-to-all-done.2), kind=kOutput, calls=%fused_computation.34 | convolution fusion | flops 2351431680 | bytes 11206656 | tf_op jit(solution)/shard_map/sjcd,jdh->sjch/dot_general | solution.py:74
  91.0 20.6 %all-to-all-done.1 = bf16[8,4,80,448]{3,2,1,0:T(8,128)(2,1)} async-done(((bf16[8,4,80,448]{3,2,1,0:T(8,128)(2,1)}), bf16[8,4,80,448]{3,2,1,0:T(8,128)(2,1)}, u32[]{:S(2)}, u32[]{:S(2)}) %all-to-all-start.1) | async-done | bytes 2293792 | tf_op jit(solution)/shard_map/all_to_all | solution.py:70
  111.5 8.0 %convert_bitcast_fusion.2 = bf16[8,4,80,1024]{3,2,0,1:T(8,128)(2,1)} fusion(bf16[4,1024,448]{1,2,0:T(8,128)(2,1)} %param.13, bf16[8,4,80,448]{3,2,1,0:T(8,128)(2,1)} %all-to-all-done.1), kind=kOutput, calls=%fused_computation.35 | convolution fusion | flops 2351431680 | bytes 11206656 | tf_op jit(solution)/shard_map/sjcd,jhd->sjch/dot_general | solution.py:75
  125.4 14.6 %scatter_custom_fusion = bf16[2560]{0:T(1024)(128)(2,1)S(1)} fusion(s32[2048]{0:T(1024)S(1)} %bitcast.75, bf16[2048]{0:T(1024)(128)(2,1)S(1)} %reshape.140, bf16[]{:T(256)} %constant.15.clone.1), kind=kCustom, calls=%fused_computation.79 | custom fusion | bytes 5122 | tf_op jit(solution)/shard_map/scatter | solution.py:59
  140.7 4.8 %all-to-all-start = ((bf16[8,4,80]{2,1,0:T(4,128)(2,1)}), bf16[8,4,80]{2,1,0:T(4,128)(2,1)S(1)}, u32[]{:S(2)}, u32[]{:S(2)}) async-start(bf16[8,4,80]{2,1,0:T(4,128)(2,1)} %reshape.97), calls=%async_computation | async-start | bytes 16384 | tf_op jit(solution)/shard_map/all_to_all | solution.py:71
  150.2 180.0 %all-reduce.5.cloned.1.call-done = (bf16[8,4,80,1024]{3,2,0,1:T(8,128)(2,1)}, bf16[8,4,80,1024]{3,2,0,1:T(8,128)(2,1)}, bf16[8,4,80,1024]{3,2,0,1:T(8,128)(2,1)}) async-done(((bf16[8,4,80,1024]{3,2,0,1:T(8,128)(2,1)}, bf16[8,4,80,1024]{3,2,0,1:T(8,128)(2,1)}, bf16[8,4,80,1024]{3,2,0,1:T(8,128)(2,1)}), (bf16[8,4,80,1024]{3,2,0,1:T(8,128)(2,1)}, bf16[8,4,80,1024]{3,2,0,1:T(8,128)(2,1)}, ...) | async-done | bytes 15728656 | tf_op jit(solution)/shard_map/psum | solution.py:81
  330.2 12.0 %fusion.2 = (bf16[8,4,80]{2,0,1:T(8,128)(2,1)S(1)}, bf16[8,4,80,1024]{3,2,0,1:T(8,128)(2,1)S(1)}, bf16[8,4,80,1024]{3,2,0,1:T(8,128)(2,1)}) fusion(bf16[8,4,80,1024]{3,2,0,1:T(8,128)(2,1)} %get-tuple-element.55, bf16[8,4,80,1024]{3,2,0,1:T(8,128)(2,1)} %get-tuple-element.54, bf16[8,4,80,1024]{3,2,0,1:T(8,128)(2,1)} %get-tuple-element.56, ...), kind=kLoop, calls=%fused_computation.15 | loop fusion | flops 52426240 | bytes 26229760 | tf_op jit(solution)/shard_map/reduce_sum | solution.py:22
  342.2 4.6 %fusion.16 = f32[4,8,80,448]{3,2,1,0:T(8,128)} fusion(bf16[8,4,80,1024]{3,2,0,1:T(8,128)(2,1)S(1)} %get-tuple-element.58, bf16[4,448,1024]{2,1,0:T(8,128)(2,1)S(1)} %copy-done.5), kind=kOutput, calls=%fused_computation.37 | convolution fusion | flops 2348810240 | bytes 13500416 | tf_op jit(solution)/shard_map/sjch,jdh->sjcd/dot_general | solution.py:97
  347.4 5.1 %all-to-all-start.4 = ((bf16[8,4,80]{2,1,0:T(4,128)(2,1)}), bf16[8,4,80]{2,1,0:T(4,128)(2,1)S(1)}, u32[]{:S(2)}, u32[]{:S(2)}) async-start(bf16[8,4,80]{2,1,0:T(4,128)(2,1)} %copy.156), calls=%async_computation.4 | async-start | bytes 16384 | tf_op jit(solution)/shard_map/all_to_all | solution.py:101
  352.5 8.1 %fusion.32 = bf16[8,4,80,448]{3,2,0,1:T(8,128)(2,1)S(1)} fusion(f32[4,8,80,448]{3,2,1,0:T(8,128)} %fusion.16, bf16[8,4,80,1024]{3,2,0,1:T(8,128)(2,1)} %get-tuple-element.59, bf16[4,448,1024]{2,1,0:T(8,128)(2,1)} %param.12), kind=kOutput, calls=%fused_computation.47 | convolution fusion | flops 2351104000 | bytes 15794176 | tf_op jit(solution)/shard_map/sjch,jdh->sjcd/dot_general | solution.py:98
  360.7 4.5 %bitcast_convert_fusion.1 = bf16[4,448,1024]{2,1,0:T(8,128)(2,1)} fusion(bf16[8,4,80,448]{3,2,1,0:T(8,128)(2,1)S(1)} %copy-done.2, bf16[8,4,80,1024]{3,2,0,1:T(8,128)(2,1)S(1)} %bitcast.68), kind=kOutput, calls=%fused_computation.25 | convolution fusion | flops 2350645248 | bytes 11206656 | tf_op jit(solution)/shard_map/sjcd,sjch->jdh/dot_general | solution.py:90
  367.0 4.8 %all-to-all-start.3 = ((bf16[8,4,80,448]{3,2,1,0:T(8,128)(2,1)}), bf16[8,4,80,448]{3,2,1,0:T(8,128)(2,1)S(1)}, u32[]{:S(2)}, u32[]{:S(2)}) async-start(bf16[8,4,80,448]{3,2,1,0:T(8,128)(2,1)} %copy.155), calls=%async_computation.3 | async-start | bytes 5242880 | tf_op jit(solution)/shard_map/all_to_all | solution.py:100
  371.8 8.2 %bitcast_convert_fusion.2 = bf16[4,448,1024]{2,1,0:T(8,128)(2,1)} fusion(bf16[8,4,80,448]{3,2,1,0:T(8,128)(2,1)} %copy-done.1, bf16[8,4,80,1024]{3,2,0,1:T(8,128)(2,1)} %copy-done), kind=kOutput, calls=%fused_computation.26 | convolution fusion | flops 2350645248 | bytes 11206656 | tf_op jit(solution)/shard_map/sjcd,sjch->jdh/dot_general | solution.py:87
  380.0 10.1 %bitcast_convert_fusion = bf16[4,1024,448]{1,2,0:T(8,128)(2,1)} fusion(bf16[8,4,80,1024]{3,2,0,1:T(8,128)(2,1)} %get-tuple-element.54, f32[8,4,80]{2,0,1:T(8,128)S(1)} %copy_convert_fusion, bf16[8,4,80,448]{3,2,1,0:T(8,128)(2,1)} %all-to-all-done.1, bf16[8,4,80,1024]{3,2,0,1:T(8,128)(2,1)} %get-tuple-element.56), kind=kOutput, calls=%fused_computation.24 | convolution fusion | flops 2374238208 | bytes 16459776 | tf_op jit(solution)/shard_map/sjch,sjcd->jhd/dot_general | solution.py:93
  390.1 13.1 %gather_fusion.3 = bf16[2048]{0:T(1024)(128)(2,1)S(1)} fusion(bf16[2560]{0:T(1024)(128)(2,1)S(1)} %reshape.102, s32[2048]{0:T(1024)S(1)} %broadcast_clamp_fusion), kind=kCustom, calls=%fused_computation.3 | custom fusion | bytes 16384 | tf_op jit(solution)/shard_map/gather | solution.py:108
  404.0 9.1 %gather_fusion.2 = bf16[2048,448]{1,0:T(8,128)(2,1)} fusion(bf16[2560,448]{1,0:T(8,128)(2,1)S(1)} %bitcast.66, s32[2048]{0:T(1024)S(1)} %broadcast_clamp_fusion), kind=kCustom, calls=%fused_computation.2 | custom fusion | bytes 3678208 | tf_op jit(solution)/shard_map/gather | solution.py:104
  (63 shorter events, 22.4 us)
Async XLA Ops:
  36.5 5.9 %copy-start.3 = (bf16[256,448]{0,1:T(8,128)(2,1)S(1)}, bf16[256,448]{0,1:T(8,128)(2,1)}, u32[]{:S(2)}) copy-start(bf16[256,448]{0,1:T(8,128)(2,1)} %param.8) | copy-start | bytes 688132
  36.5 37.7 %all-to-all-start.2 = ((bf16[8,4,80,448]{3,2,1,0:T(8,128)(2,1)}), bf16[8,4,80,448]{3,2,1,0:T(8,128)(2,1)S(1)}, u32[]{:S(2)}, u32[]{:S(2)}) async-start(bf16[8,4,80,448]{3,2,1,0:T(8,128)(2,1)} %bitcast.9), calls=%async_computation.2 | async-start | bytes 5242880 | tf_op jit(solution)/shard_map/all_to_all | solution.py:69
  74.3 12.1 %copy-start.1 = (bf16[8,4,80,448]{3,2,1,0:T(8,128)(2,1)}, bf16[8,4,80,448]{3,2,1,0:T(8,128)(2,1)S(1)}, u32[]{:S(2)}) copy-start(bf16[8,4,80,448]{3,2,1,0:T(8,128)(2,1)S(1)} %all-to-all-done.2) | copy-start | bytes 6881284
  74.3 37.2 %all-to-all-start.1 = ((bf16[8,4,80,448]{3,2,1,0:T(8,128)(2,1)}), bf16[8,4,80,448]{3,2,1,0:T(8,128)(2,1)}, u32[]{:S(2)}, u32[]{:S(2)}) async-start(bf16[8,4,80,448]{3,2,1,0:T(8,128)(2,1)} %bitcast.5), calls=%async_computation.1 | async-start | bytes 5242880 | tf_op jit(solution)/shard_map/all_to_all | solution.py:70
  79.6 250.7 %all-reduce.5.cloned.1.call-start = ((), (), s32[]{:S(2)}) async-start(), calls=%async_computation.6 | async-start | bytes 31457280 | tf_op jit(solution)/shard_map/psum | solution.py:81
  79.6 6.8 %copy-start.6 = (bf16[4,448,1024]{2,1,0:T(8,128)(2,1)S(1)}, bf16[4,448,1024]{2,1,0:T(8,128)(2,1)}, u32[]{:S(2)}) copy-start(bf16[4,448,1024]{2,1,0:T(8,128)(2,1)} %param.12) | copy-start | bytes 11010052
  119.5 0.7 copy-start.4
  121.2 19.5 %all-to-all-start.5 = ((f32[8,1,32]{2,1,0:T(1,128)}), f32[8,1,32]{2,1,0:T(1,128)S(1)}, u32[]{:S(2)}, u32[]{:S(2)}) async-start(f32[8,1,32]{2,1,0:T(1,128)} %broadcast_in_dim.11), calls=%async_computation.5 | async-start | bytes 8192 | tf_op jit(solution)/shard_map/all_to_all | solution.py:9
  140.7 9.5 %all-to-all-start = ((bf16[8,4,80]{2,1,0:T(4,128)(2,1)}), bf16[8,4,80]{2,1,0:T(4,128)(2,1)S(1)}, u32[]{:S(2)}, u32[]{:S(2)}) async-start(bf16[8,4,80]{2,1,0:T(4,128)(2,1)} %reshape.97), calls=%async_computation | async-start | bytes 16384 | tf_op jit(solution)/shard_map/all_to_all | solution.py:71
  330.2 12.0 %copy-start.5 = (bf16[4,448,1024]{2,1,0:T(8,128)(2,1)S(1)}, bf16[4,448,1024]{2,1,0:T(8,128)(2,1)}, u32[]{:S(2)}) copy-start(bf16[4,448,1024]{2,1,0:T(8,128)(2,1)} %param.11) | copy-start | bytes 11010052
  342.2 4.7 %copy-start = (bf16[8,4,80,1024]{3,2,0,1:T(8,128)(2,1)}, bf16[8,4,80,1024]{3,2,0,1:T(8,128)(2,1)S(1)}, u32[]{:S(2)}) copy-start(bf16[8,4,80,1024]{3,2,0,1:T(8,128)(2,1)S(1)} %get-tuple-element.58) | copy-start | bytes 15728644
  342.2 18.5 %slice-start = ((s8[5242880]{0:T(1024)(128)(4,1)}), s8[1048576]{0:T(1024)(128)(4,1)S(1)}, s32[]{:S(2)}) async-start(s8[5242880]{0:T(1024)(128)(4,1)} %bitcast.67), calls=%async_computation.7 | async-start | bytes 2097152
  347.4 19.5 %all-to-all-start.4 = ((bf16[8,4,80]{2,1,0:T(4,128)(2,1)}), bf16[8,4,80]{2,1,0:T(4,128)(2,1)S(1)}, u32[]{:S(2)}, u32[]{:S(2)}) async-start(bf16[8,4,80]{2,1,0:T(4,128)(2,1)} %copy.156), calls=%async_computation.4 | async-start | bytes 16384 | tf_op jit(solution)/shard_map/all_to_all | solution.py:101
  352.5 8.1 %slice-start.1 = ((s8[5242880]{0:T(1024)(128)(4,1)}), s8[4194304]{0:T(1024)(128)(4,1)S(1)}, s32[]{:S(2)}) async-start(s8[5242880]{0:T(1024)(128)(4,1)} %bitcast.67), calls=%async_computation.8 | async-start | bytes 8388608
  352.5 8.2 %copy-start.2 = (bf16[8,4,80,448]{3,2,1,0:T(8,128)(2,1)S(1)}, bf16[8,4,80,448]{3,2,1,0:T(8,128)(2,1)}, u32[]{:S(2)}) copy-start(bf16[8,4,80,448]{3,2,1,0:T(8,128)(2,1)} %copy-done.1) | copy-start | bytes 6881284
  367.0 37.0 %all-to-all-start.3 = ((bf16[8,4,80,448]{3,2,1,0:T(8,128)(2,1)}), bf16[8,4,80,448]{3,2,1,0:T(8,128)(2,1)S(1)}, u32[]{:S(2)}, u32[]{:S(2)}) async-start(bf16[8,4,80,448]{3,2,1,0:T(8,128)(2,1)} %copy.155), calls=%async_computation.3 | async-start | bytes 5242880 | tf_op jit(solution)/shard_map/all_to_all | solution.py:100
Sparse Core Ops, SparseCore 0:
  119.7 210.4 all-reduce.4
where the time goes:
time: 425 us; the launch traced here: 424 us
  waiting for transfers between devices  228 us (54%)
  local copies, waits for them, and re-layouts  70.4 us (17%)
  matrix products  55 us (13%)
  starting transfers between devices  30.1 us (7%)
  other arithmetic  25.9 us (6%)
  between operations  14.2 us (3%)
    psum x1, waiting for transfers between devices, on_device(): lax.psum(up_pre.astype(jnp.bfloat16), 'local').astype(jnp.float32)  180 us
    all_to_all x1, waiting for transfers between devices, on_device(): lax.all_to_all(send_tokens, 'node', split_axis=0, concat_axis=0, tiled=True)  23.4 us
    all_to_all x1, waiting for transfers between devices, on_device(): lax.all_to_all(send_grads, 'node', split_axis=0, concat_axis=0, tiled=True)  20.6 us
    scatter x1, local copies, waits for them, and re-layouts, on_device(): jnp.zeros((experts * capacity,), jnp.bfloat16).at[target].set(flat_gates)  14.6 us
    gather x1, local copies, waits for them, and re-layouts, on_device(): returned_products.reshape(experts * capacity)[target]  13.1 us
    reduce_sum x1, other arithmetic, activation_grads(): products = jnp.sum(hidden * back_hidden, axis=-1)  12 us
    dot_general x1, matrix products, on_device(): jnp.einsum('sjch,sjcd->jhd', weighted, grad_rows, preferred_element_type=...  10.1 us
    another operation x3, other arithmetic  9.41 us
  transfers between devices with their start and end apart: 7, of which 4 were waited for; matrix products, arithmetic and copies ran while one was open for 20% of the time, Pallas kernels for 0%

commit v1 on v0

v1 whole, which is shorter than its diff:
```python
import jax
import jax.numpy as jnp
from jax import lax
from jax.sharding import PartitionSpec as P

BF16 = jnp.bfloat16
F32 = jnp.float32


def activation_grads(gate_pre, up_pre, back_hidden, gate_col):
    logistic = jax.nn.sigmoid(gate_pre)
    swished = gate_pre * logistic
    hidden = swished * up_pre
    products = jnp.sum(hidden * back_hidden, axis=-1)
    scaled = gate_col * back_hidden
    grad_up = (scaled * swished).astype(BF16)
    grad_gate = (scaled * up_pre * logistic * (1.0 + gate_pre * (1.0 - logistic))).astype(BF16)
    weighted = (gate_col * hidden).astype(BF16)
    return weighted, grad_gate, grad_up, products


def slot_picks(named, capacity):
    count = named.shape[-1]
    earlier = jnp.arange(count)[:, None] < jnp.arange(count)[None, :]
    slot = jnp.einsum(
        "...s,st->...t", named.astype(BF16), earlier.astype(BF16), preferred_element_type=F32
    )
    slot = jnp.where(named, slot.astype(jnp.int32), -1)
    return (slot[..., None, :] == jnp.arange(capacity, dtype=jnp.int32)[:, None]).astype(BF16)


def on_device(tokens, grad_out, gates, routes, w_gate, w_up, w_down):
    nodes = lax.axis_size("node")
    me = lax.axis_index("node")
    tok_node, width = tokens.shape
    top_k = routes.shape[1]
    own = w_gate.shape[0]
    experts = own * nodes
    capacity = 5 * tok_node * top_k // (4 * experts)
    lanes = -(-(width + experts) // 128) * 128
    spare = lanes - width - experts

    expert_ids = jnp.arange(experts, dtype=jnp.int32)
    choice = routes.T[:, None, :] == expert_ids[None, :, None]
    gate_of = jnp.sum(jnp.where(choice, gates.T[:, None, :].astype(F32), 0.0), axis=0).astype(BF16)
    packed = jnp.concatenate([tokens.T, gate_of, jnp.zeros((spare, tok_node), BF16)], axis=0)
    all_tokens = lax.all_gather(packed, "node", axis=0, tiled=False)
    all_grads = lax.all_gather(grad_out.T, "node", axis=0, tiled=False)

    home_picks = slot_picks(jnp.any(choice, axis=0), capacity)

    all_gates = all_tokens[:, width : width + experts, :]
    loads = jnp.sum(all_gates.astype(F32), axis=(0, 2)) * (experts / (tok_node * top_k * 1.0))
    my_gates = lax.dynamic_slice_in_dim(all_gates, me * own, own, axis=1)
    picks = slot_picks(my_gates > 0, capacity)
    gate_col = jnp.sum(picks.astype(F32) * my_gates[:, :, None, :].astype(F32), axis=-1)
    gate_col = jnp.swapaxes(gate_col, 0, 1).reshape(own, nodes * capacity, 1)

    def rows_of(source):
        rows = jnp.einsum("bjct,bdt->jbcd", picks, source, preferred_element_type=F32)
        return rows.astype(BF16).reshape(own, nodes * capacity, width)

    token_rows = rows_of(all_tokens[:, :width, :])
    grad_rows = rows_of(all_grads)

    gate_pre = jnp.einsum("jrd,jdh->jrh", token_rows, w_gate, preferred_element_type=F32)
    up_pre = jnp.einsum("jrd,jdh->jrh", token_rows, w_up, preferred_element_type=F32)
    back = jnp.einsum("jrd,jhd->jrh", grad_rows, w_down, preferred_element_type=F32)
    gate_full, up_full, back_full = lax.psum(
        (gate_pre.astype(BF16), up_pre.astype(BF16), back.astype(BF16)), "local"
    )
    weighted, grad_gate, grad_up, products = activation_grads(
        gate_full.astype(F32), up_full.astype(F32), back_full.astype(F32), gate_col
    )
    input_rows = (
        jnp.einsum("jrh,jdh->jrd", grad_gate, w_gate, preferred_element_type=F32)
        + jnp.einsum("jrh,jdh->jrd", grad_up, w_up, preferred_element_type=F32)
    ).astype(BF16)
    expert_of = me * own + jnp.arange(own, dtype=jnp.int32)
    marks = expert_of[:, None, None] == expert_ids[None, None, :]
    product_cols = jnp.where(marks, products.astype(BF16)[..., None], jnp.zeros((), BF16))
    back_rows = jnp.concatenate(
        [input_rows, product_cols, jnp.zeros((own, nodes * capacity, spare), BF16)], axis=-1
    )
    back_rows = jnp.swapaxes(back_rows.reshape(own, nodes, capacity, lanes), 0, 1)
    returned = lax.all_to_all(back_rows, "node", split_axis=0, concat_axis=0, tiled=True)

    grad_wg = jnp.einsum(
        "jrd,jrh->jdh", token_rows, grad_gate, preferred_element_type=F32
    ).astype(BF16)
    grad_wu = jnp.einsum(
        "jrd,jrh->jdh", token_rows, grad_up, preferred_element_type=F32
    ).astype(BF16)
    grad_wd = jnp.einsum(
        "jrh,jrd->jhd", weighted, grad_rows, preferred_element_type=F32
    ).astype(BF16)

    home = jnp.einsum(
        "st,sd->dt",
        home_picks.reshape(experts * capacity, tok_node),
        returned.reshape(experts * capacity, lanes),
        preferred_element_type=F32,
    )
    grad_tokens = home[:width].astype(BF16).T
    products_home = home[width : width + experts]
    grad_gates = jnp.sum(jnp.where(choice, products_home[None], 0.0), axis=1).astype(BF16).T
    return (grad_tokens, grad_gates, grad_wg, grad_wu, grad_wd, loads)


def solution(mesh):
    in_specs = (
        P("node", "local"),
        P("node", "local"),
        P("node", None),
        P("node", None),
        P("node", "local", None),
        P("node", "local", None),
        P("node", None, "local"),
    )
    out_specs = (
        P("node", "local"),
        P("node", None),
        P("node", "local", None),
        P("node", "local", None),
        P("node", None, "local"),
        P(),
    )
    return jax.shard_map(
        on_device, mesh=mesh, in_specs=in_specs, out_specs=out_specs, check_vma=False
    )
```

time: 425 us -> 361 us (0.85)
  local copies, waits for them, and re-layouts: 70.4 us -> 11 us
  waiting for transfers between devices: 228 us -> 264 us
  starting transfers between devices: 30.1 us -> 5.38 us
  other arithmetic: 25.9 us -> 17.4 us
  matrix products: 55 us -> 49.3 us
    all_gather x0 -> x2, waiting for transfers between devices: none -> 41.5 us  [the longest x1 28.2 us: on_device(): all_tokens = lax.all_gather(packed, 'node', axis=0, tiled=False)]
    gather x4 -> x0, local copies, waits for them, and re-layouts: 38.6 us -> none  [the longest x1 13.1 us: on_device(): returned_products.reshape(experts * capacity)[target]]
    all_to_all x6 -> x1, waiting for transfers between devices: 48.2 us -> 15.5 us  [on_device(): lax.all_to_all(back_rows, 'node', split_axis=0, concat_axis=0, tiled=True)]
    psum x1, waiting for transfers between devices: 180 us -> 206 us  [on_device(): lax.psum((gate_pre.astype(BF16), up_pre.astype(BF16), back.astype(BF16)),...]
    all_to_all x6 -> x1, starting transfers between devices: 30.1 us -> 5.26 us  [on_device(): lax.all_to_all(back_rows, 'node', split_axis=0, concat_axis=0, tiled=True)]
    scatter x2 -> x0, local copies, waits for them, and re-layouts: 22.6 us -> none  [the longest x1 14.6 us: on_device(): jnp.zeros((experts * capacity,), jnp.bfloat16).at[target].set(flat_gates)]
    reduce_sum x5 -> x4, other arithmetic: 15.2 us -> 2.34 us  [the longest x1 0.73 us: on_device(): jnp.sum(jnp.where(choice, gates.T[:, None, :].astype(F32), 0.0), axis=0)]
    convert_element_type x3, other arithmetic: 0.03 us -> 12 us  [the longest x1 10.6 us: activation_grads(): (scaled * up_pre * logistic * (1.0 + gate_pre * (1.0 - logistic))).astype...]
  transfers between devices with their start and end apart: 7 -> 4, of which waited for: 4 -> 4; matrix products, arithmetic and copies ran while one was open for 20% -> 9% of each run, Pallas kernels for 0% -> 0%
where the time goes in v1:
time: 361 us
  waiting for transfers between devices  264 us (73%)
  matrix products  49.3 us (14%)
  other arithmetic  17.4 us (5%)
  between operations  14 us (4%)
  local copies, waits for them, and re-layouts  11 us (3%)
  starting transfers between devices  5.38 us (1%)
    psum x1, waiting for transfers between devices, on_device(): lax.psum((gate_pre.astype(BF16), up_pre.astype(BF16), back.astype(BF16)),...  206 us
    all_gather x1, waiting for transfers between devices, on_device(): all_tokens = lax.all_gather(packed, 'node', axis=0, tiled=False)  28.2 us
    all_to_all x1, waiting for transfers between devices, on_device(): lax.all_to_all(back_rows, 'node', split_axis=0, concat_axis=0, tiled=True)  15.5 us
    all_gather x1, waiting for transfers between devices, on_device(): all_grads = lax.all_gather(grad_out.T, 'node', axis=0, tiled=False)  13.3 us
    convert_element_type x1, other arithmetic, activation_grads(): (scaled * up_pre * logistic * (1.0 + gate_pre * (1.0 - logistic))).astype...  10.6 us
    dot_general x1, matrix products, on_device(): jnp.einsum('jrd,jrh->jdh', token_rows, grad_gate, preferred_element_type=...  8.31 us
    dot_general x1, matrix products, on_device(): jnp.einsum('jrh,jrd->jhd', weighted, grad_rows, preferred_element_type=F32)  8.11 us
  transfers between devices with their start and end apart: 4, of which 4 were waited for; matrix products, arithmetic and copies ran while one was open for 9% of the time, Pallas kernels for 0%

profile of v1, /device:TPU:1, one launch (start us, length us, event | category | flops | bytes accessed | tf_op | source)
XLA Modules:
  0.0 360.9 jit_solution(11081610462446863368)
XLA Ops:
  7.9 0.7 select_reduce_fusion.1
  8.7 1.8 maximum_maximum_fusion
  11.3 28.2 %all-gather.5.cloned.1.call-done = bf16[4096,256]{1,0:T(8,128)(2,1)} async-done(((bf16[512,256]{1,0:T(8,128)(2,1)}), bf16[4096,256]{1,0:T(8,128)(2,1)}) %all-gather.5.cloned.1.call-update) | async-done | bytes 2097168 | tf_op jit(solution)/shard_map/all_gather | solution.py:47
  39.5 0.9 slice.17
  41.2 2.5 convert_bitcast_fusion
  44.0 4.6 %convolution_convert_fusion = bf16[4,640,1024]{2,1,0:T(8,128)(2,1)} fusion(bf16[4,640,448]{2,1,0:T(8,128)(2,1)S(1)} %bitcast.58, bf16[4,448,1024]{2,1,0:T(8,128)(2,1)S(1)} %copy-done.7), kind=kOutput, calls=%fused_computation.21 | convolution fusion | flops 2351431680 | bytes 11206656 | tf_op jit(solution)/shard_map/jrd,jdh->jrh/dot_general | solution.py:66
  48.6 4.6 %convolution_convert_fusion.1 = bf16[4,640,1024]{2,1,0:T(8,128)(2,1)} fusion(bf16[4,640,448]{2,1,0:T(8,128)(2,1)S(1)} %bitcast.59, bf16[4,448,1024]{2,1,0:T(8,128)(2,1)S(1)} %copy-done.9), kind=kOutput, calls=%fused_computation.22 | convolution fusion | flops 2351431680 | bytes 11206656 | tf_op jit(solution)/shard_map/jrd,jdh->jrh/dot_general | solution.py:67
  53.2 13.3 %all-gather.7.cloned.1.call-done = bf16[3584,256]{1,0:T(8,128)(2,1)} async-done(((bf16[448,256]{1,0:T(8,128)(2,1)}), bf16[3584,256]{1,0:T(8,128)(2,1)}) %all-gather.7.cloned.1.call-update) | async-done | bytes 1835024 | tf_op jit(solution)/shard_map/all_gather | solution.py:48
  66.5 2.5 convert_bitcast_fusion.1
  69.2 1.5 copy-done.2
  70.7 4.6 %convolution_convert_fusion.2 = bf16[4,640,1024]{2,1,0:T(8,128)(2,1)} fusion(bf16[4,640,448]{2,1,0:T(8,128)(2,1)S(1)} %bitcast.62, bf16[4,1024,448]{1,2,0:T(8,128)(2,1)S(1)} %copy-done.6), kind=kOutput, calls=%fused_computation.23 | convolution fusion | flops 2351431680 | bytes 11206656 | tf_op jit(solution)/shard_map/jrd,jhd->jrh/dot_general | solution.py:68
  76.6 0.7 dynamic-slice_convert_fusion
  78.9 206.1 %all-reduce.3.cloned.1.call-done = (bf16[4,640,1024]{2,1,0:T(8,128)(2,1)}, bf16[4,640,1024]{2,1,0:T(8,128)(2,1)}, bf16[4,640,1024]{2,1,0:T(8,128)(2,1)}) async-done(((bf16[4,640,1024]{2,1,0:T(8,128)(2,1)}, bf16[4,640,1024]{2,1,0:T(8,128)(2,1)}, bf16[4,640,1024]{2,1,0:T(8,128)(2,1)}), (bf16[4,640,1024]{2,1,0:T(8,128)(2,1)}, bf16[4,640,1024]{2,1,0:T(8,128)(2,1)}, ...) | async-done | bytes 15728656 | tf_op jit(solution)/shard_map/psum | solution.py:69
  285.0 10.6 %fusion.5 = (bf16[4,640,1024]{2,1,0:T(8,128)(2,1)S(1)}, bf16[4,640]{1,0:T(4,128)(2,1)S(1)}, bf16[4,640,1024]{2,1,0:T(8,128)(2,1)S(1)}) fusion(bf16[4,640,1024]{2,1,0:T(8,128)(2,1)} %get-tuple-element.7, bf16[4,640,1024]{2,1,0:T(8,128)(2,1)} %get-tuple-element.6, bf16[4,640,1024]{2,1,0:T(8,128)(2,1)} %get-tuple-element.8, f32[4,640]{1,0:T(4,128)S(1)} %mul.61), kind=kLoop, calls=%fused_computation.12 | loop fusion | flops 52426240 | bytes 26229760 | tf_op jit(solution)/shard_map/convert_element_type | solution.py:17
  295.6 3.0 fusion.29
  298.7 4.7 %convolution_convert_fusion.3 = bf16[4,448,1024]{2,1,0:T(8,128)(2,1)} fusion(bf16[4,640,448]{2,1,0:T(8,128)(2,1)S(1)} %bitcast.60, bf16[4,640,1024]{2,1,0:T(8,128)(2,1)S(1)} %get-tuple-element.11), kind=kOutput, calls=%fused_computation.34 | convolution fusion | flops 2350645248 | bytes 11206656 | tf_op jit(solution)/shard_map/jrd,jrh->jdh/dot_general | solution.py:91
  303.4 3.3 add_convert_fusion
  307.1 2.6 copy.65
  309.7 3.4 copy.66
  313.2 5.3 %all-to-all-start = ((bf16[8,4,80,512]{3,2,1,0:T(8,128)(2,1)}), bf16[8,4,80,512]{3,2,1,0:T(8,128)(2,1)}, u32[]{:S(2)}, u32[]{:S(2)}) async-start(bf16[8,4,80,512]{3,2,1,0:T(8,128)(2,1)} %copy.66), calls=%async_computation | async-start | bytes 5242880 | tf_op jit(solution)/shard_map/all_to_all | solution.py:86
  318.4 8.3 %convolution_convert_fusion.4 = bf16[4,448,1024]{2,1,0:T(8,128)(2,1)} fusion(bf16[4,640,448]{2,1,0:T(8,128)(2,1)} %bitcast.61, bf16[4,640,1024]{2,1,0:T(8,128)(2,1)} %copy-done), kind=kOutput, calls=%fused_computation.35 | convolution fusion | flops 2350645248 | bytes 11206656 | tf_op jit(solution)/shard_map/jrd,jrh->jdh/dot_general | solution.py:88
  326.8 8.1 %fusion.15 = bf16[4,1024,448]{1,2,0:T(8,128)(2,1)} fusion(bf16[4,640,448]{2,1,0:T(8,128)(2,1)S(1)} %bitcast.63, bf16[4,640,1024]{2,1,0:T(8,128)(2,1)S(1)} %bitcast.57, f32[4,640]{1,0:T(4,128)S(1)} %mul.61, bf16[4,640,1024]{2,1,0:T(8,128)(2,1)} %get-tuple-element.8), kind=kOutput, calls=%fused_computation.33 | convolution fusion | flops 2374238208 | bytes 16459776 | tf_op jit(solution)/shard_map/jrh,jrd->jhd/dot_general | solution.py:94
  334.9 15.5 %all-to-all-done = bf16[8,4,80,512]{3,2,1,0:T(8,128)(2,1)} async-done(((bf16[8,4,80,512]{3,2,1,0:T(8,128)(2,1)}), bf16[8,4,80,512]{3,2,1,0:T(8,128)(2,1)}, u32[]{:S(2)}, u32[]{:S(2)}) %all-to-all-start) | async-done | bytes 2621472 | tf_op jit(solution)/shard_map/all_to_all | solution.py:86
  350.4 2.6 fusion.30
  (57 shorter events, 7.4 us)
Async XLA Ops:
  7.2 32.4 %all-gather.5.cloned.1.call-start = ((), (), s32[]{:S(2)}) async-start(), calls=%async_computation.1 | async-start | bytes 2359296 | tf_op jit(solution)/shard_map/all_gather | solution.py:47
  10.5 56.0 %all-gather.7.cloned.1.call-start = ((), (), s32[]{:S(2)}) async-start(), calls=%async_computation.2 | async-start | bytes 2064384 | tf_op jit(solution)/shard_map/all_gather | solution.py:48
  11.3 273.7 %all-reduce.3.cloned.1.call-start = ((), (), s32[]{:S(2)}) async-start(), calls=%async_computation.3 | async-start | bytes 31457280 | tf_op jit(solution)/shard_map/psum | solution.py:69
  40.5 0.7 copy-start.4
  41.2 2.8 copy-start.7
  44.0 254.7 %copy-start.1 = (bf16[4,8,80,448]{3,2,1,0:T(8,128)(2,1)}, bf16[4,8,80,448]{3,2,1,0:T(8,128)(2,1)S(1)}, u32[]{:S(2)}) copy-start(bf16[4,8,80,448]{3,2,1,0:T(8,128)(2,1)S(1)} %copy.62) | copy-start | bytes 6881284
  44.0 4.6 %copy-start.9 = (bf16[4,448,1024]{2,1,0:T(8,128)(2,1)S(1)}, bf16[4,448,1024]{2,1,0:T(8,128)(2,1)}, u32[]{:S(2)}) copy-start(bf16[4,448,1024]{2,1,0:T(8,128)(2,1)} %param.12) | copy-start | bytes 11010052
  66.5 4.2 %copy-start.6 = (bf16[4,1024,448]{1,2,0:T(8,128)(2,1)S(1)}, bf16[4,1024,448]{1,2,0:T(8,128)(2,1)}, u32[]{:S(2)}) copy-start(bf16[4,1024,448]{1,2,0:T(8,128)(2,1)} %param.13) | copy-start | bytes 11010052
  69.2 1.5 copy-start.2
  75.2 0.7 copy-start.5
  285.0 10.6 %copy-start.8 = (bf16[4,448,1024]{2,1,0:T(8,128)(2,1)S(1)}, bf16[4,448,1024]{2,1,0:T(8,128)(2,1)}, u32[]{:S(2)}) copy-start(bf16[4,448,1024]{2,1,0:T(8,128)(2,1)} %param.11) | copy-start | bytes 11010052
  295.6 3.1 copy-start
  298.7 4.8 %copy-start.10 = (bf16[4,448,1024]{2,1,0:T(8,128)(2,1)S(1)}, bf16[4,448,1024]{2,1,0:T(8,128)(2,1)}, u32[]{:S(2)}) copy-start(bf16[4,448,1024]{2,1,0:T(8,128)(2,1)} %param.12) | copy-start | bytes 11010052
  313.2 13.6 %slice-start = ((s8[5242880]{0:T(1024)(128)(4,1)}), s8[1048576]{0:T(1024)(128)(4,1)S(1)}, s32[]{:S(2)}) async-start(s8[5242880]{0:T(1024)(128)(4,1)} %bitcast.56), calls=%async_computation.4 | async-start | bytes 2097152
  313.2 37.2 %all-to-all-start = ((bf16[8,4,80,512]{3,2,1,0:T(8,128)(2,1)}), bf16[8,4,80,512]{3,2,1,0:T(8,128)(2,1)}, u32[]{:S(2)}, u32[]{:S(2)}) async-start(bf16[8,4,80,512]{3,2,1,0:T(8,128)(2,1)} %copy.66), calls=%async_computation | async-start | bytes 5242880 | tf_op jit(solution)/shard_map/all_to_all | solution.py:86
  318.4 8.3 %slice-start.1 = ((s8[5242880]{0:T(1024)(128)(4,1)}), s8[4194304]{0:T(1024)(128)(4,1)S(1)}, s32[]{:S(2)}) async-start(s8[5242880]{0:T(1024)(128)(4,1)} %bitcast.56), calls=%async_computation.5 | async-start | bytes 8388608
  318.4 8.3 %copy-start.3 = (bf16[4,8,80,448]{3,2,1,0:T(8,128)(2,1)S(1)}, bf16[4,8,80,448]{3,2,1,0:T(8,128)(2,1)}, u32[]{:S(2)}) copy-start(bf16[4,8,80,448]{3,2,1,0:T(8,128)(2,1)} %copy-done.2) | copy-start | bytes 6881284
Sparse Core Ops, SparseCore 0:
  10.6 28.8 all-gather.4
  41.2 25.2 all-gather.6
  75.4 209.5 all-reduce.2

commit v2 on v1

v2 whole, which is shorter than its diff:
```python
import jax
import jax.numpy as jnp
from jax import lax
from jax.experimental import pallas as pl
from jax.experimental.pallas import tpu as pltpu
from jax.sharding import PartitionSpec as P

BF16 = jnp.bfloat16
F32 = jnp.float32


def activation_grads(gate_pre, up_pre, back_hidden, gate_col):
    logistic = jax.nn.sigmoid(gate_pre)
    swished = gate_pre * logistic
    hidden = swished * up_pre
    products = jnp.sum(hidden * back_hidden, axis=-1)
    scaled = gate_col * back_hidden
    grad_up = (scaled * swished).astype(BF16)
    grad_gate = (scaled * up_pre * logistic * (1.0 + gate_pre * (1.0 - logistic))).astype(BF16)
    weighted = (gate_col * hidden).astype(BF16)
    return weighted, grad_gate, grad_up, products


def slot_picks(named, capacity):
    count = named.shape[-1]
    earlier = jnp.arange(count)[:, None] < jnp.arange(count)[None, :]
    slot = jnp.einsum(
        "...s,st->...t", named.astype(BF16), earlier.astype(BF16), preferred_element_type=F32
    )
    slot = jnp.where(named, slot.astype(jnp.int32), -1)
    return (slot[..., None, :] == jnp.arange(capacity, dtype=jnp.int32)[:, None]).astype(BF16)


def forward_body(tokens_ref, grads_ref, gate_ref, up_ref, down_ref, out_ref):
    quarters, _, rows, lanes = out_ref.shape
    for kind, (left, right) in enumerate(
        ((tokens_ref, gate_ref), (tokens_ref, up_ref), (grads_ref, down_ref))
    ):
        part = jnp.dot(left[0], right[0], preferred_element_type=F32).astype(BF16)
        out_ref[:, kind] = part.reshape(quarters, rows, lanes)


def forward(token_rows, grad_rows, w_gate, w_up, w_down_t, quarters):
    own, slots, width = token_rows.shape
    hidden = w_gate.shape[2]
    lanes = hidden // 2
    share = slots // quarters
    rows = pl.BlockSpec((1, slots, width), lambda e, h: (e, 0, 0))
    weight = pl.BlockSpec((1, width, lanes), lambda e, h: (e, 0, h))
    return pl.pallas_call(
        forward_body,
        grid=(own, hidden // lanes),
        in_specs=[rows, rows, weight, weight, weight],
        out_specs=pl.BlockSpec((quarters, 3, share, lanes), lambda e, h: (e, 0, 0, h)),
        out_shape=jax.ShapeDtypeStruct((own * quarters, 3, share, hidden), BF16),
        name="forward",
    )(token_rows, grad_rows, w_gate, w_up, w_down_t)


def rows_body(grad_gate_ref, grad_up_ref, gate_ref, up_ref, cols_ref, out_ref):
    nodes, _, capacity, _ = out_ref.shape
    slots, extra = cols_ref.shape[1:]
    width = gate_ref.shape[1]
    hidden = gate_ref.shape[2]
    total = jnp.zeros((slots, width), F32)
    for left, right in ((grad_gate_ref, gate_ref), (grad_up_ref, up_ref)):
        total += lax.dot_general(
            left[...].reshape(slots, hidden),
            right[0],
            (((1,), (1,)), ((), ())),
            preferred_element_type=F32,
        )
    out_ref[:, 0, :, :width] = total.astype(BF16).reshape(nodes, capacity, width)
    out_ref[:, 0, :, width:] = cols_ref[0].reshape(nodes, capacity, extra)


def back_rows_of(first, w_gate, w_up, cols, nodes, quarters):
    own, width, hidden = w_gate.shape
    slots, extra = cols.shape[1:]
    share, capacity = slots // quarters, slots // nodes
    grads = [
        pl.BlockSpec((quarters, share, hidden), lambda e, kind=kind: (e, kind, 0))
        for kind in range(2)
    ]
    weight = pl.BlockSpec((1, width, hidden), lambda e: (e, 0, 0))
    return pl.pallas_call(
        rows_body,
        grid=(own,),
        in_specs=[*grads, weight, weight, pl.BlockSpec((1, slots, extra), lambda e: (e, 0, 0))],
        out_specs=pl.BlockSpec((nodes, 1, capacity, width + extra), lambda e: (0, e, 0, 0)),
        out_shape=jax.ShapeDtypeStruct((nodes, own, capacity, width + extra), BF16),
        name="back_rows",
    )(first, first, w_gate, w_up, cols)


def weight_body(rows_ref, *refs):
    half = len(refs) // 2
    for grad_ref, out_ref in zip(refs[:half], refs[half:]):
        slots = rows_ref.shape[1]
        out_ref[0] = lax.dot_general(
            rows_ref[0],
            grad_ref[...].reshape(slots, grad_ref.shape[-1]),
            (((0,), (0,)), ((), ())),
            preferred_element_type=F32,
        ).astype(BF16)


def weight_grads(rows, grads, kinds, quarters):
    own, slots, width = rows.shape
    hidden = grads.shape[-1]
    share = slots // quarters
    lanes = hidden // 2
    out = pl.BlockSpec((1, width, lanes), lambda e, h: (e, 0, h))
    return pl.pallas_call(
        weight_body,
        grid=(own, hidden // lanes),
        in_specs=[pl.BlockSpec((1, slots, width), lambda e, h: (e, 0, 0))]
        + [
            pl.BlockSpec((quarters, share, lanes), lambda e, h, kind=kind: (e, kind, h))
            for kind in range(kinds)
        ],
        out_specs=[out] * kinds,
        out_shape=[jax.ShapeDtypeStruct((own, width, hidden), BF16)] * kinds,
        name="weight_grads",
    )(rows, *([grads] * kinds))


def on_device(tokens, grad_out, gates, routes, w_gate, w_up, w_down):
    nodes = lax.axis_size("node")
    me = lax.axis_index("node")
    tok_node, width = tokens.shape
    top_k = routes.shape[1]
    own = w_gate.shape[0]
    hidden = w_gate.shape[2]
    experts = own * nodes
    capacity = 5 * tok_node * top_k // (4 * experts)
    lanes = -(-(width + experts) // 128) * 128
    spare = lanes - width - experts
    slots = nodes * capacity

    expert_ids = jnp.arange(experts, dtype=jnp.int32)
    choice = routes.T[:, None, :] == expert_ids[None, :, None]
    gate_of = jnp.sum(jnp.where(choice, gates.T[:, None, :].astype(F32), 0.0), axis=0).astype(BF16)
    packed = jnp.concatenate([tokens.T, gate_of, jnp.zeros((spare, tok_node), BF16)], axis=0)
    all_tokens = lax.all_gather(packed, "node", axis=0, tiled=False)
    all_grads = lax.all_to_all(
        jnp.broadcast_to(grad_out.T[None], (nodes, width, tok_node)), "node", 0, 0, tiled=True
    )

    home_picks = slot_picks(jnp.any(choice, axis=0), capacity)

    all_gates = all_tokens[:, width : width + experts, :]
    loads = jnp.sum(all_gates.astype(F32), axis=(0, 2)) * (experts / (tok_node * top_k * 1.0))
    my_gates = lax.dynamic_slice_in_dim(all_gates, me * own, own, axis=1)
    picks = slot_picks(my_gates > 0, capacity)
    gate_col = jnp.sum(picks.astype(F32) * my_gates[:, :, None, :].astype(F32), axis=-1)
    gate_col = jnp.swapaxes(gate_col, 0, 1).reshape(own, slots, 1)

    def rows_of(chosen, source):
        rows = jnp.einsum("bjct,bdt->jbcd", chosen, source, preferred_element_type=F32)
        return rows.astype(BF16).reshape(chosen.shape[1], slots, width)

    devices = lax.axis_size("local")
    place = lax.axis_index("local")
    quarters = devices // own
    share = slots // quarters
    token_rows = rows_of(picks, all_tokens[:, :width, :])
    grad_rows = rows_of(picks, all_grads)
    parts = forward(token_rows, grad_rows, w_gate, w_up, jnp.swapaxes(w_down, 1, 2), quarters)
    parts = parts.reshape(devices, 3 * share, hidden)
    sums = lax.psum_scatter(parts, "local", scatter_dimension=0, tiled=True)
    sums = sums.reshape(3, share, hidden).astype(F32)
    my_gate = lax.dynamic_slice_in_dim(gate_col.reshape(own * slots, 1), place * share, share)
    weighted, grad_gate, grad_up, products = activation_grads(sums[0], sums[1], sums[2], my_gate)
    products = jnp.pad(products.astype(BF16)[None], ((0, 15), (0, hidden - share)))
    first = jnp.concatenate([grad_gate, grad_up, products], axis=0)
    first = lax.all_gather(first, "local", axis=0, tiled=False)
    last = lax.all_gather(weighted, "local", axis=0, tiled=False)

    products = first[:, 2 * share, :share].reshape(own, slots)
    expert_of = me * own + jnp.arange(own, dtype=jnp.int32)
    marks = expert_of[:, None, None] == jnp.arange(experts + spare, dtype=jnp.int32)
    cols = jnp.where(marks, products[..., None], jnp.zeros((), BF16))
    back_rows = back_rows_of(first, w_gate, w_up, cols, nodes, quarters)
    returned = lax.all_to_all(back_rows, "node", split_axis=0, concat_axis=0, tiled=True)
    grad_wg, grad_wu = weight_grads(token_rows, first, 2, quarters)
    home = jnp.einsum(
        "st,sd->dt",
        home_picks.reshape(experts * capacity, tok_node),
        returned.reshape(experts * capacity, lanes),
        preferred_element_type=F32,
    )
    last, grad_wg, grad_wu, home = lax.optimization_barrier((last, grad_wg, grad_wu, home))
    (grad_wd,) = weight_grads(grad_rows, last, 1, quarters)
    grad_wd = jnp.swapaxes(grad_wd, 1, 2)
    grad_tokens = home[:width].astype(BF16).T
    products_home = home[width : width + experts]
    grad_gates = jnp.sum(jnp.where(choice, products_home[None], 0.0), axis=1).astype(BF16).T
    return (grad_tokens, grad_gates, grad_wg, grad_wu, grad_wd, loads)


def solution(mesh):
    in_specs = (
        P("node", "local"),
        P("node", "local"),
        P("node", None),
        P("node", None),
        P("node", "local", None),
        P("node", "local", None),
        P("node", None, "local"),
    )
    out_specs = (
        P("node", "local"),
        P("node", None),
        P("node", "local", None),
        P("node", "local", None),
        P("node", None, "local"),
        P(),
    )
    return jax.shard_map(
        on_device, mesh=mesh, in_specs=in_specs, out_specs=out_specs, check_vma=False
    )
```

time: 361 us -> 341 us (0.945)
  Pallas kernels: 0 us -> 50.6 us
  matrix products: 49.3 us -> 5.2 us
  waiting for transfers between devices: 264 us -> 239 us
  other arithmetic: 17.4 us -> 10.8 us
  starting transfers between devices: 5.38 us -> 11.1 us
    psum x1 -> x0, waiting for transfers between devices: 206 us -> none  [on_device(): lax.psum((gate_pre.astype(BF16), up_pre.astype(BF16), back.astype(BF16)),...]
    unnamed x3 -> x5, waiting for transfers between devices: 0.73 us -> 105 us
    all_gather x1 -> x2, waiting for transfers between devices: 13.3 us -> 87.9 us  [the longest x1 81.3 us: on_device(): first = lax.all_gather(first, 'local', axis=0, tiled=False)]
    pallas_call x0 -> x4, Pallas kernels: none -> 50.6 us  [the longest x2 21.7 us: weight_grads(): pl.pallas_call(weight_body, grid=(own, hidden // lanes), in_specs=[pl.Blo...]
    dot_general x10 -> x2, matrix products: 46.4 us -> 3.22 us  [rows_of(): jnp.einsum('bjct,bdt->jbcd', chosen, source, preferred_element_type=F32)]
    convert_element_type x1, other arithmetic: 10.6 us -> 0.47 us  [activation_grads(): (scaled * up_pre * logistic * (1.0 + gate_pre * (1.0 - logistic))).astype...]
    all_to_all x0 -> x1, starting transfers between devices: none -> 5.79 us  [on_device(): lax.all_to_all(jnp.broadcast_to(grad_out.T[None], (nodes, width, tok_node...]
  transfers between devices with their start and end apart: 4 -> 6, of which waited for: 4 -> 5; matrix products, arithmetic and copies ran while one was open for 9% -> 4% of each run, Pallas kernels for 0% -> 7%
where the time goes in v2:
time: 341 us; the launch traced here: 340 us
  waiting for transfers between devices  239 us (70%)
  Pallas kernels  50.6 us (15%)
  between operations  13.9 us (4%)
  starting transfers between devices  11.1 us (3%)
  other arithmetic  10.8 us (3%)
  local copies, waits for them, and re-layouts  9.74 us (3%)
  matrix products  5.2 us (2%)
    unnamed x5, waiting for transfers between devices  105 us
    all_gather x1, waiting for transfers between devices, on_device(): first = lax.all_gather(first, 'local', axis=0, tiled=False)  81.3 us
    all_gather x1, waiting for transfers between devices, on_device(): all_tokens = lax.all_gather(packed, 'node', axis=0, tiled=False)  28 us
    pallas_call x2, Pallas kernels, weight_grads(): pl.pallas_call(weight_body, grid=(own, hidden // lanes), in_specs=[pl.Blo...  21.7 us
    pallas_call x1, Pallas kernels, forward(): pl.pallas_call(forward_body, grid=(own, hidden // lanes), in_specs=[rows,...  18.4 us
    all_to_all x1, waiting for transfers between devices, on_device(): lax.all_to_all(back_rows, 'node', split_axis=0, concat_axis=0, tiled=True)  18 us
    pallas_call x1, Pallas kernels, back_rows_of(): pl.pallas_call(rows_body, grid=(own,), in_specs=[*grads, weight, weight,...  10.5 us
  transfers between devices with their start and end apart: 6, of which 5 were waited for; matrix products, arithmetic and copies ran while one was open for 4% of the time, Pallas kernels for 7%

profile of v2, /device:TPU:1, one launch (start us, length us, event | category | flops | bytes accessed | tf_op | source)
XLA Modules:
  0.0 340.0 jit_solution(14630090122830499744)
XLA Ops:
  8.7 1.8 maximum_maximum_fusion
  10.5 2.3 broadcast_in_dim.79
  12.8 5.8 %all-to-all-start = ((bf16[8,448,256]{2,1,0:T(8,128)(2,1)}), bf16[8,448,256]{2,1,0:T(8,128)(2,1)S(1)}, u32[]{:S(2)}, u32[]{:S(2)}) async-start(bf16[8,448,256]{2,1,0:T(8,128)(2,1)} %broadcast_in_dim.79), calls=%async_computation | async-start | bytes 3670016 | tf_op jit(solution)/shard_map/all_to_all | solution.py:146
  18.6 28.0 %all-gather.8.cloned.1.call-done = bf16[4096,256]{1,0:T(8,128)(2,1)} async-done(((bf16[512,256]{1,0:T(8,128)(2,1)}), bf16[4096,256]{1,0:T(8,128)(2,1)}) %all-gather.8.cloned.1.call-update) | async-done | bytes 2097168 | tf_op jit(solution)/shard_map/all_gather | solution.py:145
  46.6 0.9 slice.36
  47.8 2.4 convert_bitcast_fusion.1
  50.1 1.7 copy.33
  52.7 1.7 copy.34
  54.5 18.4 %forward.1 = bf16[16,3,160,1024]{3,2,1,0:T(8,128)(2,1)} custom-call(bf16[4,640,448]{2,1,0:T(8,128)(2,1)} %bitcast.93, bf16[4,640,448]{2,1,0:T(8,128)(2,1)} %bitcast.95, bf16[4,448,1024]{2,1,0:T(8,128)(2,1)} %gate_ref.3, bf16[4,448,1024]{2,1,0:T(8,128)(2,1)} %up_ref.3, bf16[4,448,1024]{2,1,0:T(8,128)(2,1)} %bitcast.98), custom_call_target="tpu_custom_call" | custom-call | tf_op jit(solution)/shard_map/forward/pallas_call | solution.py:50
  73.8 104.8 %reduce-scatter.4.cloned.1.call-done = bf16[1,480,1024]{2,1,0:T(8,128)(2,1)} async-done(((bf16[16,480,1024]{2,1,0:T(8,128)(2,1)}), bf16[1,480,1024]{2,1,0:T(8,128)(2,1)}) %reduce-scatter.4.cloned.1.call-update) | async-done | bytes 983056
  178.6 1.4 convert_element_type.94
  180.5 0.9 fusion.9
  181.4 0.9 multiply_convert_fusion.1
  182.5 81.3 %all-gather.10.cloned.1.call-done = bf16[5376,1024]{1,0:T(8,128)(2,1)} async-done(((bf16[336,1024]{1,0:T(8,128)(2,1)}), bf16[5376,1024]{1,0:T(8,128)(2,1)}) %all-gather.10.cloned.1.call-update) | async-done | bytes 11010064 | tf_op jit(solution)/shard_map/all_gather | solution.py:177
  263.8 0.9 slice_reduce_fusion
  264.8 1.2 broadcast_select_fusion.cols_ref
  266.0 10.5 %back_rows.1 = bf16[8,4,80,512]{3,2,1,0:T(8,128)(2,1)} custom-call(bf16[16,336,1024]{2,1,0:T(8,128)(2,1)} %bitcast.88, bf16[16,336,1024]{2,1,0:T(8,128)(2,1)} %bitcast.89, bf16[4,448,1024]{2,1,0:T(8,128)(2,1)} %gate_ref.3, bf16[4,448,1024]{2,1,0:T(8,128)(2,1)} %up_ref.3, bf16[4,640,64]{2,1,0:T(8,128)(2,1)} %broadcast_select_fusion.cols_ref), custom_call_target="tpu_custom_call" | custom-call | tf_op jit(solution)/shard_map/back_rows/pallas_call | solution.py:86
  276.5 5.2 %all-to-all-start.1 = ((bf16[8,4,80,512]{3,2,1,0:T(8,128)(2,1)}), bf16[8,4,80,512]{3,2,1,0:T(8,128)(2,1)S(1)}, u32[]{:S(2)}, u32[]{:S(2)}) async-start(bf16[8,4,80,512]{3,2,1,0:T(8,128)(2,1)} %back_rows.1), calls=%async_computation.1 | async-start | bytes 5242880 | tf_op jit(solution)/shard_map/all_to_all | solution.py:185
  283.2 12.4 %weight_grads.2 = (bf16[4,448,1024]{2,1,0:T(8,128)(2,1)}, bf16[4,448,1024]{2,1,0:T(8,128)(2,1)}) custom-call(bf16[4,640,448]{2,1,0:T(8,128)(2,1)} %bitcast.94, bf16[16,336,1024]{2,1,0:T(8,128)(2,1)} %bitcast.90, bf16[16,336,1024]{2,1,0:T(8,128)(2,1)} %bitcast.91), custom_call_target="tpu_custom_call" | custom-call | tf_op jit(solution)/shard_map/weight_grads/pallas_call | solution.py:114
  295.6 18.0 %all-to-all-done.1 = bf16[8,4,80,512]{3,2,1,0:T(8,128)(2,1)S(1)} async-done(((bf16[8,4,80,512]{3,2,1,0:T(8,128)(2,1)}), bf16[8,4,80,512]{3,2,1,0:T(8,128)(2,1)S(1)}, u32[]{:S(2)}, u32[]{:S(2)}) %all-to-all-start.1) | async-done | bytes 2621472 | tf_op jit(solution)/shard_map/all_to_all | solution.py:185
  313.6 1.7 fusion.29
  315.3 6.6 %all-gather.6.cloned.1.call-done.refs_0_ = bf16[16,160,1024]{2,1,0:T(8,128)(2,1)} async-done(((bf16[1,160,1024]{2,1,0:T(8,128)(2,1)}), bf16[16,160,1024]{2,1,0:T(8,128)(2,1)}) %all-gather.6.cloned.1.call-update) | async-done | bytes 5242896 | tf_op jit(solution)/shard_map/all_gather | solution.py:178
  321.8 1.7 fusion.23
  323.6 9.2 %weight_grads.3 = bf16[4,448,1024]{2,1,0:T(8,128)(2,1)} custom-call(bf16[4,640,448]{2,1,0:T(8,128)(2,1)} %bitcast.96, bf16[16,160,1024]{2,1,0:T(8,128)(2,1)} %all-gather.6.cloned.1.call-done.refs_0_), custom_call_target="tpu_custom_call" | custom-call | tf_op jit(solution)/shard_map/weight_grads/pallas_call | solution.py:114
  (38 shorter events, 6.3 us)
Async XLA Ops:
  7.2 39.4 %all-gather.8.cloned.1.call-start = ((), (), s32[]{:S(2)}) async-start(), calls=%async_computation.4 | async-start | bytes 2359296 | tf_op jit(solution)/shard_map/all_gather | solution.py:145
  12.8 39.0 %all-to-all-start = ((bf16[8,448,256]{2,1,0:T(8,128)(2,1)}), bf16[8,448,256]{2,1,0:T(8,128)(2,1)S(1)}, u32[]{:S(2)}, u32[]{:S(2)}) async-start(bf16[8,448,256]{2,1,0:T(8,128)(2,1)} %broadcast_in_dim.79), calls=%async_computation | async-start | bytes 3670016 | tf_op jit(solution)/shard_map/all_to_all | solution.py:146
  18.6 160.0 %reduce-scatter.4.cloned.1.call-start = ((), (), s32[]{:S(2)}) async-start(), calls=%async_computation.6 | async-start | bytes 16711680
  72.8 190.9 %all-gather.10.cloned.1.call-start = ((), (), s32[]{:S(2)}) async-start(), calls=%async_computation.5 | async-start | bytes 11698176 | tf_op jit(solution)/shard_map/all_gather | solution.py:177
  181.4 140.5 %all-gather.6.cloned.1.call-start = ((), (), s32[]{:S(2)}) async-start(), calls=%async_computation.3 | async-start | bytes 5570560 | tf_op jit(solution)/shard_map/all_gather | solution.py:178
  276.5 5.2 %copy-start = (s32[256,8]{0,1:T(8,128)S(1)}, s32[256,8]{0,1:T(8,128)}, u32[]{:S(2)}) copy-start(s32[256,8]{0,1:T(8,128)} %param.10) | copy-start | bytes 24580
  276.5 37.0 %all-to-all-start.1 = ((bf16[8,4,80,512]{3,2,1,0:T(8,128)(2,1)}), bf16[8,4,80,512]{3,2,1,0:T(8,128)(2,1)S(1)}, u32[]{:S(2)}, u32[]{:S(2)}) async-start(bf16[8,4,80,512]{3,2,1,0:T(8,128)(2,1)} %back_rows.1), calls=%async_computation.1 | async-start | bytes 5242880 | tf_op jit(solution)/shard_map/all_to_all | solution.py:185
  323.6 9.2 %slice-start = ((f32[512,256]{1,0:T(8,128)}), f32[32,256]{1,0:T(8,128)S(1)}, s32[]{:S(2)}) async-start(f32[512,256]{1,0:T(8,128)} %fusion.29), calls=%async_computation.7 | async-start | bytes 65536 | tf_op jit(solution)/shard_map/slice | solution.py:197
Sparse Core Ops, SparseCore 0:
  10.6 35.8 all-gather.7
  73.0 105.5 reduce-scatter.3
  181.5 82.2 all-gather.9
  265.8 55.9 all-gather.5

commit v3 on v2

--- a/solution.py
+++ b/solution.py
@@ -7,6 +7,12 @@
 
 BF16 = jnp.bfloat16
 F32 = jnp.float32
+
+
+def copy_for_each(array, axis, groups=None):
+    devices = len(groups[0]) if groups else lax.axis_size(axis)
+    copies = jnp.broadcast_to(array[None], (devices, *array.shape))
+    return lax.all_to_all(copies, axis, 0, 0, tiled=True, axis_index_groups=groups)
 
 
 def activation_grads(gate_pre, up_pre, back_hidden, gate_col):
@@ -36,22 +42,22 @@
     for kind, (left, right) in enumerate(
         ((tokens_ref, gate_ref), (tokens_ref, up_ref), (grads_ref, down_ref))
     ):
-        part = jnp.dot(left[0], right[0], preferred_element_type=F32).astype(BF16)
+        slots = left[...].reshape(quarters * rows, left.shape[-1])
+        part = jnp.dot(slots, right[0], preferred_element_type=F32).astype(BF16)
         out_ref[:, kind] = part.reshape(quarters, rows, lanes)
 
 
 def forward(token_rows, grad_rows, w_gate, w_up, w_down_t, quarters):
-    own, slots, width = token_rows.shape
+    nodes, own, capacity, width = token_rows.shape
     hidden = w_gate.shape[2]
-    lanes = hidden // 2
-    share = slots // quarters
-    rows = pl.BlockSpec((1, slots, width), lambda e, h: (e, 0, 0))
-    weight = pl.BlockSpec((1, width, lanes), lambda e, h: (e, 0, h))
+    share = nodes * capacity // quarters
+    rows = pl.BlockSpec((nodes, 1, capacity, width), lambda e: (0, e, 0, 0))
+    weight = pl.BlockSpec((1, width, hidden), lambda e: (e, 0, 0))
     return pl.pallas_call(
         forward_body,
-        grid=(own, hidden // lanes),
+        grid=(own,),
         in_specs=[rows, rows, weight, weight, weight],
-        out_specs=pl.BlockSpec((quarters, 3, share, lanes), lambda e, h: (e, 0, 0, h)),
+        out_specs=pl.BlockSpec((quarters, 3, share, hidden), lambda e: (e, 0, 0, 0)),
         out_shape=jax.ShapeDtypeStruct((own * quarters, 3, share, hidden), BF16),
         name="forward",
     )(token_rows, grad_rows, w_gate, w_up, w_down_t)
@@ -96,27 +102,23 @@
 def weight_body(rows_ref, *refs):
     half = len(refs) // 2
     for grad_ref, out_ref in zip(refs[:half], refs[half:]):
-        slots = rows_ref.shape[1]
-        out_ref[0] = lax.dot_general(
-            rows_ref[0],
-            grad_ref[...].reshape(slots, grad_ref.shape[-1]),
-            (((0,), (0,)), ((), ())),
-            preferred_element_type=F32,
+        slots = rows_ref.shape[2]
+        out_ref[0] = jnp.dot(
+            rows_ref[0], grad_ref[...].reshape(slots, grad_ref.shape[-1]), preferred_element_type=F32
         ).astype(BF16)
 
 
 def weight_grads(rows, grads, kinds, quarters):
-    own, slots, width = rows.shape
+    own, width, slots = rows.shape
     hidden = grads.shape[-1]
     share = slots // quarters
-    lanes = hidden // 2
-    out = pl.BlockSpec((1, width, lanes), lambda e, h: (e, 0, h))
+    out = pl.BlockSpec((1, width, hidden), lambda e: (e, 0, 0))
     return pl.pallas_call(
         weight_body,
-        grid=(own, hidden // lanes),
-        in_specs=[pl.BlockSpec((1, slots, width), lambda e, h: (e, 0, 0))]
+        grid=(own,),
+        in_specs=[pl.BlockSpec((1, width, slots), lambda e: (e, 0, 0))]
         + [
-            pl.BlockSpec((quarters, share, lanes), lambda e, h, kind=kind: (e, kind, h))
+            pl.BlockSpec((quarters, share, hidden), lambda e, kind=kind: (e, kind, 0))
             for kind in range(kinds)
         ],
         out_specs=[out] * kinds,
@@ -143,9 +145,11 @@
     gate_of = jnp.sum(jnp.where(choice, gates.T[:, None, :].astype(F32), 0.0), axis=0).astype(BF16)
     packed = jnp.concatenate([tokens.T, gate_of, jnp.zeros((spare, tok_node), BF16)], axis=0)
     all_tokens = lax.all_gather(packed, "node", axis=0, tiled=False)
-    all_grads = lax.all_to_all(
-        jnp.broadcast_to(grad_out.T[None], (nodes, width, tok_node)), "node", 0, 0, tiled=True
-    )
+    chips = [list(range(core, nodes, 2)) for core in range(2)]
+    same = copy_for_each(grad_out.T, "node", chips)
+    other = lax.ppermute(same, "node", [(n, n ^ 1) for n in range(nodes)])
+    all_grads = jnp.where(me % 2 == 0, jnp.stack([same, other], 1), jnp.stack([other, same], 1))
+    all_grads = all_grads.reshape(nodes, width, tok_node)
 
     home_picks = slot_picks(jnp.any(choice, axis=0), capacity)
 
@@ -157,8 +161,8 @@
     gate_col = jnp.swapaxes(gate_col, 0, 1).reshape(own, slots, 1)
 
     def rows_of(chosen, source):
-        rows = jnp.einsum("bjct,bdt->jbcd", chosen, source, preferred_element_type=F32)
-        return rows.astype(BF16).reshape(chosen.shape[1], slots, width)
+        rows = jnp.einsum("bjct,bdt->bjcd", chosen, source, preferred_element_type=F32)
+        return rows.astype(BF16)
 
     devices = lax.axis_size("local")
     place = lax.axis_index("local")
@@ -172,30 +176,33 @@
     sums = sums.reshape(3, share, hidden).astype(F32)
     my_gate = lax.dynamic_slice_in_dim(gate_col.reshape(own * slots, 1), place * share, share)
     weighted, grad_gate, grad_up, products = activation_grads(sums[0], sums[1], sums[2], my_gate)
-    products = jnp.pad(products.astype(BF16)[None], ((0, 15), (0, hidden - share)))
-    first = jnp.concatenate([grad_gate, grad_up, products], axis=0)
+    first = jnp.concatenate([grad_gate, grad_up], axis=0)
     first = lax.all_gather(first, "local", axis=0, tiled=False)
     last = lax.all_gather(weighted, "local", axis=0, tiled=False)
-
-    products = first[:, 2 * share, :share].reshape(own, slots)
+    products = copy_for_each(products.astype(BF16)[None], "local").reshape(own, slots)
     expert_of = me * own + jnp.arange(own, dtype=jnp.int32)
     marks = expert_of[:, None, None] == jnp.arange(experts + spare, dtype=jnp.int32)
     cols = jnp.where(marks, products[..., None], jnp.zeros((), BF16))
     back_rows = back_rows_of(first, w_gate, w_up, cols, nodes, quarters)
     returned = lax.all_to_all(back_rows, "node", split_axis=0, concat_axis=0, tiled=True)
-    grad_wg, grad_wu = weight_grads(token_rows, first, 2, quarters)
+    def columns_of(rows):
+        return jnp.transpose(rows, (1, 3, 0, 2)).reshape(own, width, slots)
+
+    grad_wg, grad_wu = weight_grads(columns_of(token_rows), first, 2, quarters)
     home = jnp.einsum(
         "st,sd->dt",
         home_picks.reshape(experts * capacity, tok_node),
         returned.reshape(experts * capacity, lanes),
         preferred_element_type=F32,
     )
-    last, grad_wg, grad_wu, home = lax.optimization_barrier((last, grad_wg, grad_wu, home))
-    (grad_wd,) = weight_grads(grad_rows, last, 1, quarters)
-    grad_wd = jnp.swapaxes(grad_wd, 1, 2)
     grad_tokens = home[:width].astype(BF16).T
     products_home = home[width : width + experts]
     grad_gates = jnp.sum(jnp.where(choice, products_home[None], 0.0), axis=1).astype(BF16).T
+    last, grad_wg, grad_wu, grad_tokens, grad_gates = lax.optimization_barrier(
+        (last, grad_wg, grad_wu, grad_tokens, grad_gates)
+    )
+    (grad_wd,) = weight_grads(columns_of(grad_rows), last, 1, quarters)
+    grad_wd = jnp.swapaxes(grad_wd, 1, 2)
     return (grad_tokens, grad_gates, grad_wg, grad_wu, grad_wd, loads)
 
 

time: 341 us -> 326 us (0.956)
  waiting for transfers between devices: 239 us -> 195 us
  blocking collectives: 0 us -> 18.7 us
  Pallas kernels: 50.6 us -> 43.1 us
  local copies, waits for them, and re-layouts: 9.74 us -> 17 us
  starting transfers between devices: 11.1 us -> 15.2 us
  matrix products: 5.2 us -> 9.18 us
    all_gather x1, waiting for transfers between devices: 28 us -> 1.16 us  [on_device(): all_tokens = lax.all_gather(packed, 'node', axis=0, tiled=False)]
    all_to_all x0 -> x1, blocking collectives: none -> 18.7 us  [copy_for_each(): lax.all_to_all(copies, axis, 0, 0, tiled=True, axis_index_groups=groups)]
    all_gather x1, waiting for transfers between devices: 81.3 us -> 65.5 us  [on_device(): first = lax.all_gather(first, 'local', axis=0, tiled=False)]
    all_to_all x1, waiting for transfers between devices: 18 us -> 7.93 us  [on_device(): lax.all_to_all(back_rows, 'node', split_axis=0, concat_axis=0, tiled=True)]
    reshape x0 -> x2, local copies, waits for them, and re-layouts: none -> 8.91 us  [columns_of(): return jnp.transpose(rows, (1, 3, 0, 2)).reshape(own, width, slots)]
    pallas_call x3, Pallas kernels: 40 us -> 32.6 us  [the longest x2 17.3 us: weight_grads(): pl.pallas_call(weight_body, grid=(own,), in_specs=[pl.BlockSpec((1, width...]
    all_to_all x1, waiting for transfers between devices: 0.01 us -> 6.38 us  [copy_for_each(): lax.all_to_all(copies, axis, 0, 0, tiled=True, axis_index_groups=groups)]
    ppermute x0 -> x1, starting transfers between devices: none -> 4.64 us  [on_device(): other = lax.ppermute(same, 'node', [(n, n ^ 1) for n in range(nodes)])]
  transfers between devices with their start and end apart: 6 -> 7, of which waited for: 5 -> 7; matrix products, arithmetic and copies ran while one was open for 4% -> 7% of each run, Pallas kernels for 7% -> 6%
where the time goes in v3:
time: 326 us; the launch traced here: 325 us
  waiting for transfers between devices  195 us (60%)
  Pallas kernels  43.1 us (13%)
  blocking collectives  18.7 us (6%)
  local copies, waits for them, and re-layouts  17 us (5%)
  starting transfers between devices  15.2 us (5%)
  between operations  13.9 us (4%)
  other arithmetic  12.6 us (4%)
  matrix products  9.18 us (3%)
    unnamed x5, waiting for transfers between devices  106 us
    all_gather x1, waiting for transfers between devices, on_device(): first = lax.all_gather(first, 'local', axis=0, tiled=False)  65.5 us
    all_to_all x1, blocking collectives, copy_for_each(): lax.all_to_all(copies, axis, 0, 0, tiled=True, axis_index_groups=groups)  18.7 us
    pallas_call x2, Pallas kernels, weight_grads(): pl.pallas_call(weight_body, grid=(own,), in_specs=[pl.BlockSpec((1, width...  17.3 us
    pallas_call x1, Pallas kernels, forward(): pl.pallas_call(forward_body, grid=(own,), in_specs=[rows, rows, weight, w...  15.3 us
    pallas_call x1, Pallas kernels, back_rows_of(): pl.pallas_call(rows_body, grid=(own,), in_specs=[*grads, weight, weight,...  10.5 us
    reshape x2, local copies, waits for them, and re-layouts, columns_of(): return jnp.transpose(rows, (1, 3, 0, 2)).reshape(own, width, slots)  8.91 us
    all_to_all x1, waiting for transfers between devices, on_device(): lax.all_to_all(back_rows, 'node', split_axis=0, concat_axis=0, tiled=True)  7.93 us
  transfers between devices with their start and end apart: 7, of which 7 were waited for; matrix products, arithmetic and copies ran while one was open for 7% of the time, Pallas kernels for 6%

profile of v3, /device:TPU:1, one launch (start us, length us, event | category | flops | bytes accessed | tf_op | source)
XLA Modules:
  0.0 324.9 jit_solution(6834662917831734200)
XLA Ops:
  8.7 1.8 maximum_maximum_fusion
  11.6 18.7 %all_to_all.15 = bf16[4,448,256]{2,1,0:T(8,128)(2,1)S(1)} all-to-all(bf16[4,448,256]{2,1,0:T(8,128)(2,1)S(1)} %broadcast_in_dim.83), channel_id=1, replica_groups={{0,32,64,96},{16,48,80,112},{1,33,65,97},{17,49,81,113},{2,34,66,98},{1..., dimensions={0} | all-to-all | bytes 1835008 | tf_op jit(solution)/shard_map/all_to_all | solution.py:15
  30.3 4.6 %collective-permute-start = (bf16[4,448,256]{2,1,0:T(8,128)(2,1)S(1)}, bf16[4,448,256]{2,1,0:T(8,128)(2,1)S(1)}, u32[]{:S(2)}, u32[]{:S(2)}) collective-permute-start(bf16[4,448,256]{2,1,0:T(8,128)(2,1)S(1)} %all_to_all.15), channel_id=1, source_target_pairs={{0,16},{16,0},{32,48},{48,32},{64,80},{80,64},{96,112},{112,96},{1... | collective-permute-start | bytes 2752520 | tf_op jit(solution)/shard_map/ppermute | solution.py:150
  34.9 2.4 collective-permute-done
  38.2 1.7 maximum_select_fusion
  42.3 3.9 %fusion.3.tokens_ref = bf16[8,4,80,448]{3,2,1,0:T(8,128)(2,1)} fusion(bf16[8,512,256]{2,1,0:T(8,128)(2,1)} %bitcast.112, s32[8,4,256]{2,1,0:T(4,128)S(1)} %copy.42), kind=kOutput, calls=%fused_computation.6 | convolution fusion | flops 589004800 | bytes 4161536 | tf_op jit(solution)/shard_map/bjct,bdt->bjcd/dot_general | solution.py:164
  46.1 2.4 fusion.4.grads_ref
  48.5 15.3 %forward.1 = bf16[16,3,160,1024]{3,2,1,0:T(8,128)(2,1)} custom-call(bf16[8,4,80,448]{3,2,1,0:T(8,128)(2,1)} %fusion.3.tokens_ref, bf16[8,4,80,448]{3,2,1,0:T(8,128)(2,1)} %fusion.4.grads_ref, bf16[4,448,1024]{2,1,0:T(8,128)(2,1)} %gate_ref.3, bf16[4,448,1024]{2,1,0:T(8,128)(2,1)} %up_ref.3, bf16[4,448,1024]{2,1,0:T(8,128)(2,1)} %bitcast.99), custom_call_target="tpu_custom_call" | custom-call | tf_op jit(solution)/shard_map/forward/pallas_call | solution.py:56
  64.7 105.8 %reduce-scatter.4.cloned.1.call-done = bf16[1,480,1024]{2,1,0:T(8,128)(2,1)} async-done(((bf16[16,480,1024]{2,1,0:T(8,128)(2,1)}), bf16[1,480,1024]{2,1,0:T(8,128)(2,1)}) %reduce-scatter.4.cloned.1.call-update) | async-done | bytes 983056
  170.6 1.4 convert_element_type.82
  175.0 5.0 %all-to-all-start.1 = ((bf16[16,1,160]{2,1,0:T(2,128)(2,1)}), bf16[16,1,160]{2,1,0:T(2,128)(2,1)S(1)}, u32[]{:S(2)}, u32[]{:S(2)}) async-start(bf16[16,1,160]{2,1,0:T(2,128)(2,1)} %broadcast_in_dim.85), calls=%async_computation.1 | async-start | bytes 32768 | tf_op jit(solution)/shard_map/all_to_all | solution.py:15
  180.1 6.4 %all-to-all-done.1 = bf16[16,1,160]{2,1,0:T(2,128)(2,1)S(1)} async-done(((bf16[16,1,160]{2,1,0:T(2,128)(2,1)}), bf16[16,1,160]{2,1,0:T(2,128)(2,1)S(1)}, u32[]{:S(2)}, u32[]{:S(2)}) %all-to-all-start.1) | async-done | bytes 5152 | tf_op jit(solution)/shard_map/all_to_all | solution.py:15
  187.9 65.5 %all-gather.10.cloned.1.call-done = bf16[5120,1024]{1,0:T(8,128)(2,1)} async-done(((bf16[320,1024]{1,0:T(8,128)(2,1)}), bf16[5120,1024]{1,0:T(8,128)(2,1)}) %all-gather.10.cloned.1.call-update) | async-done | bytes 10485776 | tf_op jit(solution)/shard_map/all_gather | solution.py:180
  253.4 10.5 %back_rows.1 = bf16[8,4,80,512]{3,2,1,0:T(8,128)(2,1)} custom-call(bf16[16,320,1024]{2,1,0:T(8,128)(2,1)} %bitcast.88, bf16[16,320,1024]{2,1,0:T(8,128)(2,1)} %bitcast.89, bf16[4,448,1024]{2,1,0:T(8,128)(2,1)} %gate_ref.3, bf16[4,448,1024]{2,1,0:T(8,128)(2,1)} %up_ref.3, bf16[4,640,64]{2,1,0:T(8,128)(2,1)} %broadcast_select_fusion.cols_ref), custom_call_target="tpu_custom_call" | custom-call | tf_op jit(solution)/shard_map/back_rows/pallas_call | solution.py:92
  263.9 5.4 %all-to-all-start.2 = ((bf16[8,4,80,512]{3,2,1,0:T(8,128)(2,1)}), bf16[8,4,80,512]{3,2,1,0:T(8,128)(2,1)}, u32[]{:S(2)}, u32[]{:S(2)}) async-start(bf16[8,4,80,512]{3,2,1,0:T(8,128)(2,1)} %back_rows.1), calls=%async_computation.2 | async-start | bytes 5242880 | tf_op jit(solution)/shard_map/all_to_all | solution.py:187
  269.9 1.7 copy.45
  271.6 4.6 %copy.46.rows_ref = bf16[4,448,640]{2,1,0:T(8,128)(2,1)} copy(bf16[4,448,640]{1,2,0:T(8,128)(2,1)} %bitcast.94) | data formatting | bytes 4587520 | tf_op jit(solution)/shard_map/reshape | solution.py:189
  276.2 1.7 copy.47
  277.9 4.3 %copy.48.rows_ref = bf16[4,448,640]{2,1,0:T(8,128)(2,1)} copy(bf16[4,448,640]{1,2,0:T(8,128)(2,1)} %bitcast.95) | data formatting | bytes 4587520 | tf_op jit(solution)/shard_map/reshape | solution.py:189
  283.1 10.3 %weight_grads.2 = (bf16[4,448,1024]{2,1,0:T(8,128)(2,1)}, bf16[4,448,1024]{2,1,0:T(8,128)(2,1)}) custom-call(bf16[4,448,640]{2,1,0:T(8,128)(2,1)} %copy.46.rows_ref, bf16[16,320,1024]{2,1,0:T(8,128)(2,1)} %bitcast.90, bf16[16,320,1024]{2,1,0:T(8,128)(2,1)} %bitcast.91), custom_call_target="tpu_custom_call" | custom-call | tf_op jit(solution)/shard_map/weight_grads/pallas_call | solution.py:116
  293.3 7.9 %all-to-all-done.2 = bf16[8,4,80,512]{3,2,1,0:T(8,128)(2,1)} async-done(((bf16[8,4,80,512]{3,2,1,0:T(8,128)(2,1)}), bf16[8,4,80,512]{3,2,1,0:T(8,128)(2,1)}, u32[]{:S(2)}, u32[]{:S(2)}) %all-to-all-start.2) | async-done | bytes 2621472 | tf_op jit(solution)/shard_map/all_to_all | solution.py:187
  301.2 2.7 fusion.28
  305.3 6.0 %all-gather.6.cloned.1.call-done.refs_0_ = bf16[16,160,1024]{2,1,0:T(8,128)(2,1)} async-done(((bf16[1,160,1024]{2,1,0:T(8,128)(2,1)}), bf16[16,160,1024]{2,1,0:T(8,128)(2,1)}) %all-gather.6.cloned.1.call-update) | async-done | bytes 5242896 | tf_op jit(solution)/shard_map/all_gather | solution.py:181
  311.3 7.1 %weight_grads.3 = bf16[4,448,1024]{2,1,0:T(8,128)(2,1)} custom-call(bf16[4,448,640]{2,1,0:T(8,128)(2,1)} %copy.48.rows_ref, bf16[16,160,1024]{2,1,0:T(8,128)(2,1)} %all-gather.6.cloned.1.call-done.refs_0_), custom_call_target="tpu_custom_call" | custom-call | tf_op jit(solution)/shard_map/weight_grads/pallas_call | solution.py:116
  (49 shorter events, 14.0 us)
Async XLA Ops:
  7.2 33.9 %all-gather.8.cloned.1.call-start = ((), (), s32[]{:S(2)}) async-start(), calls=%async_computation.5 | async-start | bytes 2359296 | tf_op jit(solution)/shard_map/all_gather | solution.py:147
  10.5 160.0 %reduce-scatter.4.cloned.1.call-start = ((), (), s32[]{:S(2)}) async-start(), calls=%async_computation.7 | async-start | bytes 16711680
  30.3 7.0 %collective-permute-start = (bf16[4,448,256]{2,1,0:T(8,128)(2,1)S(1)}, bf16[4,448,256]{2,1,0:T(8,128)(2,1)S(1)}, u32[]{:S(2)}, u32[]{:S(2)}) collective-permute-start(bf16[4,448,256]{2,1,0:T(8,128)(2,1)S(1)} %all_to_all.15), channel_id=1, source_target_pairs={{0,16},{16,0},{32,48},{48,32},{64,80},{80,64},{96,112},{112,96},{1... | collective-permute-start | bytes 2752520 | tf_op jit(solution)/shard_map/ppermute | solution.py:150
  37.3 0.9 copy-start.2
  63.8 189.6 %all-gather.10.cloned.1.call-start = ((), (), s32[]{:S(2)}) async-start(), calls=%async_computation.6 | async-start | bytes 11141120 | tf_op jit(solution)/shard_map/all_gather | solution.py:180
  173.4 137.9 %all-gather.6.cloned.1.call-start = ((), (), s32[]{:S(2)}) async-start(), calls=%async_computation.4 | async-start | bytes 5570560 | tf_op jit(solution)/shard_map/all_gather | solution.py:181
  175.0 11.4 %all-to-all-start.1 = ((bf16[16,1,160]{2,1,0:T(2,128)(2,1)}), bf16[16,1,160]{2,1,0:T(2,128)(2,1)S(1)}, u32[]{:S(2)}, u32[]{:S(2)}) async-start(bf16[16,1,160]{2,1,0:T(2,128)(2,1)} %broadcast_in_dim.85), calls=%async_computation.1 | async-start | bytes 32768 | tf_op jit(solution)/shard_map/all_to_all | solution.py:15
  263.9 5.4 %copy-start.3 = (s32[256,8]{0,1:T(8,128)S(1)}, s32[256,8]{0,1:T(8,128)}, u32[]{:S(2)}) copy-start(s32[256,8]{0,1:T(8,128)} %param.10) | copy-start | bytes 24580
  263.9 5.9 %copy-start.1 = (bf16[8,4,80,448]{3,2,1,0:T(8,128)(2,1)S(1)}, bf16[8,4,80,448]{3,2,1,0:T(8,128)(2,1)}, u32[]{:S(2)}) copy-start(bf16[8,4,80,448]{3,2,1,0:T(8,128)(2,1)} %fusion.3.tokens_ref) | copy-start | bytes 6881284
  263.9 37.3 %all-to-all-start.2 = ((bf16[8,4,80,512]{3,2,1,0:T(8,128)(2,1)}), bf16[8,4,80,512]{3,2,1,0:T(8,128)(2,1)}, u32[]{:S(2)}, u32[]{:S(2)}) async-start(bf16[8,4,80,512]{3,2,1,0:T(8,128)(2,1)} %back_rows.1), calls=%async_computation.2 | async-start | bytes 5242880 | tf_op jit(solution)/shard_map/all_to_all | solution.py:187
  271.6 4.6 %copy-start = (bf16[8,4,80,448]{3,2,1,0:T(8,128)(2,1)S(1)}, bf16[8,4,80,448]{3,2,1,0:T(8,128)(2,1)}, u32[]{:S(2)}) copy-start(bf16[8,4,80,448]{3,2,1,0:T(8,128)(2,1)} %fusion.4.grads_ref) | copy-start | bytes 6881284
Sparse Core Ops, SparseCore 0:
  10.6 30.3 all-gather.7
  63.9 106.6 reduce-scatter.3
  173.5 79.8 all-gather.9
  255.4 55.8 all-gather.5
